TPU v7x, 256 devices: a whole 4x4x8 slice. The times are simulated.
256 devices in a mesh: dp: 16 (over y, x_hi, core), space: 16 (over x_lo, z).
Axes of the slice: x: 4 (x_hi: 2, x_lo: 2; x = x_hi * 2 + x_lo), y: 4, z: 8, core: 2. Of those that a mesh axis runs over, the one named last changes fastest.
Arguments:
- act_in: bfloat16 [16, 32, 64, 2048], P('dp', 'space'), may hold values from -6 to 6
- weight_one: bfloat16 [3, 3, 3, 32, 64], replicated, may hold values from -0.21875 to 0.21875
- bias_one: float32 [64], replicated, may hold values from -3 to 3
- weight_two: bfloat16 [3, 3, 3, 64, 128], replicated, may hold values from -0.15625 to 0.15625
- bias_two: float32 [128], replicated, may hold values from -3 to 3
- cotangent: bfloat16 [16, 16, 32, 4096], P('dp', 'space'), may hold values from -24 to 24
Outputs:
- grad_input: bfloat16 [16, 32, 64, 2048], P('dp', 'space')
- grad_w_one: float32 [3, 3, 3, 32, 64], replicated
- grad_b_one: float32 [64], replicated
- grad_w_two: float32 [3, 3, 3, 64, 128], replicated
- grad_b_two: float32 [128], replicated
All inputs are finite; a program needn't handle non-finite values.
Results may differ from a plain program's by a relative error of at most 0.01.
Values may be sent and summed in bfloat16 or wider, within the bound.
No kernel may reach another device: no remote copies, remote signals or barrier semaphores. Data moves between devices by JAX's collectives and lax.ppermute only.
A program may use at most 128 MiB of HBM per device.

v0:
```python
import math
import jax
import jax.numpy as jnp
from jax import lax
from jax.sharding import PartitionSpec as P


def padded_2(cells, sides, width):
    for axis, dim in sides:
        count = lax.axis_size(axis)
        ends = count - 1
        head = lax.slice_in_dim(cells, 0, width, axis=dim)
        tail = lax.slice_in_dim(cells, cells.shape[dim] - width, cells.shape[dim], axis=dim)
        cells = jnp.concatenate(
            [
                lax.ppermute(tail, axis, [(i, (i + 1) % count) for i in range(ends)]),
                cells,
                lax.ppermute(head, axis, [((i + 1) % count, i) for i in range(ends)]),
            ],
            axis=dim,
        )
    return cells


def forward_conv(padded, kernel):
    return lax.conv_general_dilated(
        padded,
        kernel,
        (1, 1, 1),
        ((0, 0), (1, 1), (1, 1)),
        dimension_numbers=("NDHWC", "DHWIO", "NDHWC"),
        preferred_element_type=jnp.float32,
    )


def weight_grad(padded, delta):
    return lax.conv_general_dilated(
        padded,
        delta,
        (1, 1, 1),
        ((0, 0), (1, 1), (1, 1)),
        dimension_numbers=("CDHWN", "IDHWO", "DHWNC"),
        preferred_element_type=jnp.float32,
    )


def input_grad(delta, kernel, depth_pad):
    return lax.conv_general_dilated(
        delta,
        kernel[::-1, ::-1, ::-1],
        (1, 1, 1),
        (depth_pad, (1, 1), (1, 1)),
        dimension_numbers=("NDHWC", "DHWOI", "NDHWC"),
        preferred_element_type=jnp.float32,
    )


def silu_slope(value):
    sig = jax.nn.sigmoid(value)
    return sig * (1.0 + value * (1.0 - sig))


def local(act_in, weight_one, bias_one, weight_two, bias_two, cotangent):
    samples, slab, side, merged = act_in.shape
    chan_in = weight_one.shape[3]
    chan_mid = weight_one.shape[4]
    chan_out = weight_two.shape[4]
    half = side // 2
    slab_two = slab // 2
    batch_all = samples * lax.axis_size("dp")
    depth_all = slab * lax.axis_size("space")
    scale_one = 16.0 / math.sqrt(batch_all * depth_all * side * side)
    scale_two = 1.0 / math.sqrt(batch_all * (depth_all // 2) * half * half)
    x_pad = padded_2(act_in, (("space", 1),), 1).reshape(samples, slab + 2, side, side, chan_in)
    pre_one = forward_conv(x_pad, weight_one) + bias_one
    act_one = pre_one * jax.nn.sigmoid(pre_one)
    pooled = (
        act_one.reshape(samples, slab_two, 2, half, 2, half, 2, chan_mid)
        .mean(axis=(2, 4, 6))
        .astype(jnp.bfloat16)
    )
    pool_pad = padded_2(
        pooled.reshape(samples, slab_two, half, half * chan_mid), (("space", 1),), 1
    ).reshape(samples, slab_two + 2, half, half, chan_mid)
    pre_two = forward_conv(pool_pad, weight_two) + bias_two
    cot_five = cotangent.reshape(samples, slab_two, half, half, chan_out)
    delta_two = (cot_five.astype(jnp.float32) * silu_slope(pre_two)).astype(jnp.bfloat16)
    gw_two = weight_grad(pool_pad, delta_two)
    gb_two = jnp.sum(delta_two, axis=(0, 1, 2, 3), dtype=jnp.float32)
    gw_two, gb_two = lax.psum((gw_two, gb_two), ("dp", "space"))
    delta_pad = padded_2(
        delta_two.reshape(samples, slab_two, half, half * chan_out), (("space", 1),), 1
    ).reshape(samples, slab_two + 2, half, half, chan_out)
    grad_pooled = input_grad(delta_pad, weight_two, (0, 0))
    spread = jnp.broadcast_to(
        grad_pooled[:, :, None, :, None, :, None, :],
        (samples, slab_two, 2, half, 2, half, 2, chan_mid),
    ).reshape(samples, slab, side, side, chan_mid)
    delta_one = (spread / 8.0 * silu_slope(pre_one)).astype(jnp.bfloat16)
    gw_one = weight_grad(x_pad, delta_one)
    gb_one = jnp.sum(delta_one, axis=(0, 1, 2, 3), dtype=jnp.float32)
    delta_one_pad = padded_2(
        delta_one.reshape(samples, slab, side, side * chan_mid), (("space", 1),), 1
    ).reshape(samples, slab + 2, side, side, chan_mid)
    grad_x = input_grad(delta_one_pad, weight_one, (0, 0))
    gw_one, gb_one = lax.psum((gw_one, gb_one), ("dp", "space"))
    grad_input = grad_x.astype(jnp.bfloat16).reshape(samples, slab, side, side * chan_in)
    return (
        grad_input,
        gw_one * scale_one,
        gb_one * scale_one,
        gw_two * scale_two,
        gb_two * scale_two,
    )


def solution(mesh):
    placed = (P("dp", "space", None, None), P(), P(), P(), P(), P("dp", "space", None, None))
    return jax.shard_map(
        local,
        mesh=mesh,
        in_specs=placed,
        out_specs=(P("dp", "space", None, None), P(), P(), P(), P()),
        check_vma=False,
    )
```

profile of v0, /device:TPU:1, one launch (start us, length us, event | category | flops | bytes accessed | tf_op | source)
XLA Modules:
  0.0 471.9 jit_solution(11770701972416479829)
XLA Ops:
  7.2 1.6 copy.175
  8.9 4.4 collective-permute-start
  13.3 1.3 collective-permute-start.1
  14.6 9.3 %collective-permute-done = bf16[1,1,64,2048]{2,3,1,0:T(8,128)(2,1)S(1)} collective-permute-done((bf16[1,1,64,2048]{2,3,1,0:T(8,128)(2,1)S(1)}, bf16[1,1,64,2048]{2,3,1,0:T(8,128)(2,1)S(1)}, u32[]{:S(2)}, u32[]{:S(2)}) %collective-permute-start) | collective-permute-done | bytes 262176 | tf_op jit(solution)/shard_map/ppermute | solution.py:16
  23.8 4.2 collective-permute-done.1
  28.0 1.7 pad_maximum_fusion
  29.7 1.9 pad
  31.7 6.7 %copy.179 = bf16[4,64,1,8,9,32]{5,3,4,1,0,2:T(8,128)(2,1)} copy(bf16[4,64,1,8,9,32]{1,5,4,3,0,2:T(8,128)(2,1)} %bitcast.114) | data formatting | bytes 2359296 | tf_op jit(solution)/shard_map/conv_general_dilated | solution.py:26
  38.4 1.5 slice.27
  40.0 11.3 %fusion.16 = (f32[2,64,8,9,64]{4,2,3,1,0:T(8,128)S(1)}, f32[2,64,8,9,64]{4,2,3,1,0:T(8,128)}) fusion(f32[64]{0:T(128)S(1)} %copy-done.9, pred[8,9]{0,1:T(8,128)(4,1)S(1)} %copy-done.11, bf16[3,3,3,32,64]{4,3,2,1,0:T(8,128)(2,1)S(1)} %copy-done.7, bf16[4,64,1,7,2,32]{5,3,4,1,0,2:T(8,128)(2,1)S(1)} %slice.27, bf16[4,64,1,8,9,32]{5,3,4,1,0,2:T(8,128)(2,1)} %copy.179), kind=kOutput, calls=%fused_computation.18 | convolution fusion | flops 1018822656 | bytes 6238536 | tf_op jit(solution)/shard_map/conv_general_dilated | solution.py:26
  51.3 0.9 copy.180
  52.2 2.0 slice_reduce_fusion
  54.2 3.3 reduce_sum.36
  57.7 0.3 convert_element_type.57
  57.9 4.2 collective-permute-start.2
  62.3 1.5 collective-permute-start.3
  63.8 5.5 %copy.198 = f32[2,64,8,9,64]{4,1,3,2,0:T(8,128)} copy(f32[2,64,8,9,64]{4,2,3,1,0:T(8,128)} %get-tuple-element.42) | data formatting | bytes 4718592 | tf_op jit(solution)/shard_map/mul | solution.py:60
  69.3 13.0 %copy.205 = bf16[1,4,64,64,32]{4,0,3,2,1:T(2,128)(2,1)} copy(bf16[1,4,64,64,32]{2,4,3,1,0:T(8,128)(2,1)S(1)} %bitcast.106) | data formatting | bytes 2097152 | tf_op jit(solution)/shard_map/reshape | solution.py:74
  82.3 1.2 concatenate.41
  83.6 0.5 constant_dynamic-update-slice_fusion.1
  84.1 0.6 copy_dynamic-update-slice_fusion
  84.7 1.2 concatenate.42
  86.0 0.6 constant_dynamic-update-slice_fusion
  86.6 0.9 copy.236
  87.5 0.2 pad.2.clone
  87.7 0.4 copy.188
  88.2 1.5 add_multiply_fusion.1
  89.7 0.1 copy.189
  89.9 0.8 convert_reduce_fusion.1
  90.7 0.1 reshape.106
  90.8 4.9 %collective-permute-start.4 = (bf16[1,1,32,4096]{3,2,1,0:T(8,128)(2,1)S(1)}, bf16[1,1,32,4096]{3,2,1,0:T(8,128)(2,1)S(1)}, u32[]{:S(2)}, u32[]{:S(2)}) collective-permute-start(bf16[1,1,32,4096]{3,2,1,0:T(8,128)(2,1)S(1)} %reshape.106), channel_id=1, source_target_pairs={{0,1},{1,2},{2,3},{3,4},{4,5},{5,6},{6,7},{7,8},{8,9},{9,10},{10,1... | collective-permute-start | bytes 786440 | tf_op jit(solution)/shard_map/ppermute | solution.py:16
  95.7 1.7 collective-permute-start.5
  97.4 8.1 %fusion.56 = f32[3,3,3,64,128]{4,3,2,1,0:T(8,128)} fusion(bf16[1,3,32,32,64]{4,0,3,2,1:T(2,128)(2,1)S(1)} %constant_dynamic-update-slice_fusion, bf16[1,1,32,32,128]{4,3,1,2,0:T(8,128)(2,1)S(1)} %get-tuple-element.40), kind=kOutput, calls=%fused_computation.65 | convolution fusion | flops 434307072 | bytes 1540096 | tf_op jit(solution)/shard_map/conv_general_dilated | solution.py:37
  105.7 0.3 copy.212
  106.1 0.4 copy.196
  106.6 2.5 fusion.47
  109.1 0.1 copy.197
  109.3 1.0 broadcast_in_dim.4
  110.3 0.8 fusion.17
  111.1 1.4 copy-done.2
  112.5 1.5 copy.238
  114.0 2.5 reshape.107
  116.5 2.3 fusion.71
  118.8 5.7 %collective-permute-start.6 = (bf16[1,1,64,4096]{3,2,1,0:T(8,128)(2,1)}, bf16[1,1,64,4096]{3,2,1,0:T(8,128)(2,1)}, u32[]{:S(2)}, u32[]{:S(2)}) collective-permute-start(bf16[1,1,64,4096]{3,2,1,0:T(8,128)(2,1)} %get-tuple-element.45), channel_id=1, source_target_pairs={{0,1},{1,2},{2,3},{3,4},{4,5},{5,6},{6,7},{7,8},{8,9},{9,10},{10,1... | collective-permute-start | bytes 1572872 | tf_op jit(solution)/shard_map/ppermute | solution.py:16
  124.5 1.3 collective-permute-start.7
  125.8 66.2 %fusion.18 = f32[3,3,3,32,64]{4,3,2,1,0:T(8,128)} fusion(bf16[1,4,64,64,32]{4,0,3,2,1:T(2,128)(2,1)} %copy.205, bf16[1,2,64,64,64]{4,3,2,1,0:T(8,128)(2,1)S(1)} %bitcast.108), kind=kOutput, calls=%fused_computation.25 | convolution fusion | flops 887193600 | bytes 2318336 | tf_op jit(solution)/shard_map/conv_general_dilated | solution.py:37
  192.0 2.8 convert_reduce_fusion
  194.8 83.0 %all-reduce = (f32[64]{0:T(128)S(1)}, f32[128]{0:T(128)S(1)}) all-reduce(f32[64]{0:T(128)S(1)} %convert_reduce_fusion, f32[128]{0:T(128)S(1)} %copy-done.6), channel_id=1, replica_groups=mesh['dp'=16,'space'=16] {'dp','space'}, use_global_device_ids=true, to_apply=%region_4.0 | all-reduce | flops 192 | bytes 1536 | tf_op jit(solution)/shard_map/psum | solution.py:106
  277.9 0.5 broadcast_multiply_fusion.2
  278.4 0.5 broadcast_multiply_fusion.3
  278.9 2.8 concatenate.34
  281.7 2.8 concatenate.35
  284.4 2.2 maximum_bitcast_fusion
  286.7 2.7 copy.213
  289.4 1.3 pad.6.clone
  290.7 3.0 copy.203
  293.7 0.3 slice.36
  294.0 18.1 %fusion.4 = bf16[2,64,8,9,32]{4,2,3,1,0:T(8,128)(2,1)} fusion(bf16[3,3,3,32,64]{4,3,2,1,0:T(8,128)(2,1)S(1)} %copy-done.8, bf16[4,64,1,7,2,64]{5,3,4,1,0,2:T(8,128)(2,1)S(1)} %slice.36, bf16[4,64,1,8,9,64]{5,3,4,1,0,2:T(8,128)(2,1)S(1)} %copy.203), kind=kOutput, calls=%fused_computation.6 | convolution fusion | flops 1017249792 | bytes 3518464 | tf_op jit(solution)/shard_map/conv_general_dilated | solution.py:48
  312.1 3.2 copy.204
  315.3 0.3 select_convert_fusion
  315.7 1.1 copy.208
  316.9 143.7 %all-reduce.4.cloned.1.call-done = (f32[3,3,3,32,64]{4,3,2,1,0:T(8,128)}, f32[3,3,3,64,128]{4,3,2,1,0:T(8,128)}) async-done(((f32[3,3,3,32,64]{4,3,2,1,0:T(8,128)}, f32[3,3,3,64,128]{4,3,2,1,0:T(8,128)}), (f32[3,3,3,32,64]{4,3,2,1,0:T(8,128)}, f32[3,3,3,64,128]{4,3,2,1,0:T(8,128)})) %all-reduce.4.cloned.1.call-update) | async-done | bytes 1105936 | tf_op jit(solution)/shard_map/psum | solution.py:106
  460.6 2.2 broadcast_multiply_fusion
  462.8 1.8 broadcast_multiply_fusion.1
  (52 shorter events, 1.1 us)
Async XLA Ops:
  7.2 81.0 %copy-start = (bf16[3,3,3,64,128]{4,3,2,1,0:T(8,128)(2,1)S(1)}, bf16[3,3,3,64,128]{4,3,2,1,0:T(8,128)(2,1)}, u32[]{:S(2)}) copy-start(bf16[3,3,3,64,128]{4,3,2,1,0:T(8,128)(2,1)} %param.9) | copy-start | bytes 1327108
  7.2 453.4 %all-reduce.4.cloned.1.call-start = ((), (), s32[]{:S(2)}) async-start(), calls=%async_computation | async-start | bytes 2654208 | tf_op jit(solution)/shard_map/psum | solution.py:106
  8.8 15.0 %copy-start.3 = (bf16[1,2,64,2048]{2,3,1,0:T(8,128)(2,1)}, bf16[1,2,64,2048]{2,3,1,0:T(8,128)(2,1)S(1)}, u32[]{:S(2)}) copy-start(bf16[1,2,64,2048]{2,3,1,0:T(8,128)(2,1)S(1)} %copy.175) | copy-start | bytes 1572868
  8.9 15.0 %collective-permute-start = (bf16[1,1,64,2048]{2,3,1,0:T(8,128)(2,1)S(1)}, bf16[1,1,64,2048]{2,3,1,0:T(8,128)(2,1)S(1)}, u32[]{:S(2)}, u32[]{:S(2)}) collective-permute-start(bf16[1,1,64,2048]{2,3,1,0:T(8,128)(2,1)S(1)} %get-tuple-element.47), channel_id=1, source_target_pairs={{0,1},{1,2},{2,3},{3,4},{4,5},{5,6},{6,7},{7,8},{8,9},{9,10},{10,1... | collective-permute-start | bytes 786440 | tf_op jit(solution)/shard_map/ppermute | solution.py:16
  13.3 14.7 %collective-permute-start.1 = (bf16[1,1,64,2048]{2,3,1,0:T(8,128)(2,1)S(1)}, bf16[1,1,64,2048]{2,3,1,0:T(8,128)(2,1)S(1)}, u32[]{:S(2)}, u32[]{:S(2)}) collective-permute-start(bf16[1,1,64,2048]{2,3,1,0:T(8,128)(2,1)S(1)} %get-tuple-element.48), channel_id=1, source_target_pairs={{1,0},{2,1},{3,2},{4,3},{5,4},{6,5},{7,6},{8,7},{9,8},{10,9},{11,1... | collective-permute-start | bytes 786440 | tf_op jit(solution)/shard_map/ppermute | solution.py:18
  31.7 8.3 %copy-start.7 = (bf16[3,3,3,32,64]{4,3,2,1,0:T(8,128)(2,1)S(1)}, bf16[3,3,3,32,64]{4,3,2,1,0:T(8,128)(2,1)}, u32[]{:S(2)}) copy-start(bf16[3,3,3,32,64]{4,3,2,1,0:T(8,128)(2,1)} %param.7) | copy-start | bytes 331780
  31.7 8.3 %copy-start.9 = (f32[64]{0:T(128)S(1)}, f32[64]{0:T(128)}, u32[]{:S(2)}) copy-start(f32[64]{0:T(128)} %param.8) | copy-start | bytes 772
  31.7 8.3 %copy-start.11 = (pred[8,9]{0,1:T(8,128)(4,1)S(1)}, pred[8,9]{0,1:T(8,128)(4,1)}, u32[]{:S(2)}) copy-start(pred[8,9]{0,1:T(8,128)(4,1)} %constant.38) | copy-start | bytes 220
  52.2 10.0 %copy-start.4 = (bf16[1,1,32,4096]{3,2,1,0:T(8,128)(2,1)S(1)}, bf16[1,1,32,4096]{3,2,1,0:T(8,128)(2,1)}, u32[]{:S(2)}) copy-start(bf16[1,1,32,4096]{3,2,1,0:T(8,128)(2,1)} %param.11) | copy-start | bytes 786436
  57.9 24.4 %collective-permute-start.2 = (bf16[1,1,32,2048]{3,2,1,0:T(8,128)(2,1)S(1)}, bf16[1,1,32,2048]{3,2,1,0:T(8,128)(2,1)}, u32[]{:S(2)}, u32[]{:S(2)}) collective-permute-start(bf16[1,1,32,2048]{3,2,1,0:T(8,128)(2,1)S(1)} %convert_element_type.57), channel_id=1, source_target_pairs={{0,1},{1,2},{2,3},{3,4},{4,5},{5,6},{6,7},{7,8},{8,9},{9,10},{10,1... | collective-permute-start | bytes 393224 | tf_op jit(solution)/shard_map/ppermute | solution.py:16
  62.3 22.4 %collective-permute-start.3 = (bf16[1,1,32,2048]{3,2,1,0:T(8,128)(2,1)S(1)}, bf16[1,1,32,2048]{3,2,1,0:T(8,128)(2,1)}, u32[]{:S(2)}, u32[]{:S(2)}) collective-permute-start(bf16[1,1,32,2048]{3,2,1,0:T(8,128)(2,1)S(1)} %convert_element_type.57), channel_id=1, source_target_pairs={{1,0},{2,1},{3,2},{4,3},{5,4},{6,5},{7,6},{8,7},{9,8},{10,9},{11,1... | collective-permute-start | bytes 393224 | tf_op jit(solution)/shard_map/ppermute | solution.py:18
  84.7 3.5 copy-start.10
  84.7 3.5 copy-start.12
  90.8 14.6 %collective-permute-start.4 = (bf16[1,1,32,4096]{3,2,1,0:T(8,128)(2,1)S(1)}, bf16[1,1,32,4096]{3,2,1,0:T(8,128)(2,1)S(1)}, u32[]{:S(2)}, u32[]{:S(2)}) collective-permute-start(bf16[1,1,32,4096]{3,2,1,0:T(8,128)(2,1)S(1)} %reshape.106), channel_id=1, source_target_pairs={{0,1},{1,2},{2,3},{3,4},{4,5},{5,6},{6,7},{7,8},{8,9},{9,10},{10,1... | collective-permute-start | bytes 786440 | tf_op jit(solution)/shard_map/ppermute | solution.py:16
  95.7 9.8 %collective-permute-start.5 = (bf16[1,1,32,4096]{3,2,1,0:T(8,128)(2,1)S(1)}, bf16[1,1,32,4096]{3,2,1,0:T(8,128)(2,1)S(1)}, u32[]{:S(2)}, u32[]{:S(2)}) collective-permute-start(bf16[1,1,32,4096]{3,2,1,0:T(8,128)(2,1)S(1)} %reshape.106), channel_id=1, source_target_pairs={{1,0},{2,1},{3,2},{4,3},{5,4},{6,5},{7,6},{8,7},{9,8},{10,9},{11,1... | collective-permute-start | bytes 786440 | tf_op jit(solution)/shard_map/ppermute | solution.py:18
  106.5 3.8 slice-start
  106.6 3.7 slice-start.1
  111.1 1.4 copy-start.2
  118.8 160.1 %collective-permute-start.6 = (bf16[1,1,64,4096]{3,2,1,0:T(8,128)(2,1)}, bf16[1,1,64,4096]{3,2,1,0:T(8,128)(2,1)}, u32[]{:S(2)}, u32[]{:S(2)}) collective-permute-start(bf16[1,1,64,4096]{3,2,1,0:T(8,128)(2,1)} %get-tuple-element.45), channel_id=1, source_target_pairs={{0,1},{1,2},{2,3},{3,4},{4,5},{5,6},{6,7},{7,8},{8,9},{9,10},{10,1... | collective-permute-start | bytes 1572872 | tf_op jit(solution)/shard_map/ppermute | solution.py:16
  124.5 157.2 %collective-permute-start.7 = (bf16[1,1,64,4096]{3,2,1,0:T(8,128)(2,1)}, bf16[1,1,64,4096]{3,2,1,0:T(8,128)(2,1)}, u32[]{:S(2)}, u32[]{:S(2)}) collective-permute-start(bf16[1,1,64,4096]{3,2,1,0:T(8,128)(2,1)} %get-tuple-element.46), channel_id=1, source_target_pairs={{1,0},{2,1},{3,2},{4,3},{5,4},{6,5},{7,6},{8,7},{9,8},{10,9},{11,1... | collective-permute-start | bytes 1572872 | tf_op jit(solution)/shard_map/ppermute | solution.py:18
  125.7 69.1 %copy-start.6 = (f32[128]{0:T(128)S(1)}, f32[128]{0:T(128)}, u32[]{:S(2)}) copy-start(f32[128]{0:T(128)} %get-tuple-element.39) | copy-start | bytes 1540
  290.7 3.3 copy-start.8
  294.0 21.3 %copy-start.5 = (pred[8,9]{1,0:T(8,128)(4,1)S(1)}, pred[8,9]{1,0:T(8,128)(4,1)}, u32[]{:S(2)}) copy-start(pred[8,9]{1,0:T(8,128)(4,1)} %constant.34) | copy-start | bytes 220
  312.1 152.5 %copy-start.1 = (bf16[3,3,3,64,128]{4,3,2,1,0:T(8,128)(2,1)S(1)}, bf16[3,3,3,64,128]{4,3,2,1,0:T(8,128)(2,1)}, u32[]{:S(2)}) copy-start(bf16[3,3,3,64,128]{4,3,2,1,0:T(8,128)(2,1)} %param.9) | copy-start | bytes 1327108
Sparse Core Ops, SparseCore 0:
  194.9 265.5 all-reduce.3
where the time goes:
time: 481 us; the launch traced here: 472 us
  waiting for transfers between devices  157 us (33%)
  matrix products  108 us (22%)
  blocking collectives  83 us (17%)
  local copies, waits for them, and re-layouts  64.9 us (13%)
  starting transfers between devices  25 us (5%)
  other arithmetic  19.1 us (4%)
  between operations  15 us (3%)
    psum x1, waiting for transfers between devices, local(): gw_one, gb_one = lax.psum((gw_one, gb_one), ('dp', 'space'))  144 us
    psum x1, blocking collectives, local(): gw_one, gb_one = lax.psum((gw_one, gb_one), ('dp', 'space'))  83 us
    conv_general_dilated x2, matrix products, weight_grad(): lax.conv_general_dilated(padded, delta, (1, 1, 1), ((0, 0), (1, 1), (1, 1...  74.3 us
    conv_general_dilated x2, matrix products, input_grad(): lax.conv_general_dilated(delta, kernel[::-1, ::-1, ::-1], (1, 1, 1), (dep...  20.6 us
    ppermute x4, starting transfers between devices, padded_2(): lax.ppermute(tail, axis, [(i, (i + 1) % count) for i in range(ends)])  19.2 us
    reshape x2, local copies, waits for them, and re-layouts, local(): padded_2(act_in, (('space', 1),), 1)  15 us
    conv_general_dilated x2, matrix products, forward_conv(): lax.conv_general_dilated(padded, kernel, (1, 1, 1), ((0, 0), (1, 1), (1,...  12.8 us
    concatenate x8, local copies, waits for them, and re-layouts, padded_2(): jnp.concatenate([lax.ppermute(tail, axis, [(i, (i + 1) % count) for i in...  10.2 us
  transfers between devices with their start and end apart: 9, of which 3 were waited for; matrix products, arithmetic and copies ran while one was open for 29% of the time, Pallas kernels for 0%

commit v1 on v0

--- a/solution.py
+++ b/solution.py
@@ -103,7 +103,7 @@
         delta_one.reshape(samples, slab, side, side * chan_mid), (("space", 1),), 1
     ).reshape(samples, slab + 2, side, side, chan_mid)
     grad_x = input_grad(delta_one_pad, weight_one, (0, 0))
-    gw_one, gb_one = lax.psum((gw_one, gb_one), ("dp", "space"))
+    gw_one, gb_one = lax.psum(lax.psum((gw_one, gb_one), "dp"), "space")
     grad_input = grad_x.astype(jnp.bfloat16).reshape(samples, slab, side, side * chan_in)
     return (
         grad_input,

time: 481 us -> 876 us (1.82)
  the two profiles are of different devices: /device:TPU:1 before, /device:TPU:8 now
where the time goes in v1:
time: 876 us; the launch traced here: 867 us
  waiting for transfers between devices  472 us (54%)
  blocking collectives  149 us (17%)
  matrix products  125 us (14%)
  local copies, waits for them, and re-layouts  63.9 us (7%)
  starting transfers between devices  24 us (3%)
  other arithmetic  18.7 us (2%)
  between operations  14.6 us (2%)
    psum x1, waiting for transfers between devices, local(): gw_two, gb_two = lax.psum((gw_two, gb_two), ('dp', 'space'))  267 us
    psum x2, waiting for transfers between devices, local(): gw_one, gb_one = lax.psum(lax.psum((gw_one, gb_one), 'dp'), 'space')  191 us
    conv_general_dilated x2, matrix products, weight_grad(): lax.conv_general_dilated(padded, delta, (1, 1, 1), ((0, 0), (1, 1), (1, 1...  91.8 us
    psum x1, blocking collectives, local(): gw_two, gb_two = lax.psum((gw_two, gb_two), ('dp', 'space'))  79.7 us
    psum x2, blocking collectives, local(): gw_one, gb_one = lax.psum(lax.psum((gw_one, gb_one), 'dp'), 'space')  68.9 us
    conv_general_dilated x2, matrix products, input_grad(): lax.conv_general_dilated(delta, kernel[::-1, ::-1, ::-1], (1, 1, 1), (dep...  20.5 us
    ppermute x4, starting transfers between devices, padded_2(): lax.ppermute(tail, axis, [(i, (i + 1) % count) for i in range(ends)])  18.1 us
  transfers between devices with their start and end apart: 11, of which 5 were waited for; matrix products, arithmetic and copies ran while one was open for 5% of the time, Pallas kernels for 0%

profile of v1, /device:TPU:8, one launch (start us, length us, event | category | flops | bytes accessed | tf_op | source)
XLA Modules:
  0.0 867.0 jit_solution(10501670810367410610)
XLA Ops:
  7.2 1.6 copy.175
  8.9 3.9 collective-permute-start
  12.7 1.3 collective-permute-start.1
  14.0 9.8 %collective-permute-done = bf16[1,1,64,2048]{2,3,1,0:T(8,128)(2,1)S(1)} collective-permute-done((bf16[1,1,64,2048]{2,3,1,0:T(8,128)(2,1)S(1)}, bf16[1,1,64,2048]{2,3,1,0:T(8,128)(2,1)S(1)}, u32[]{:S(2)}, u32[]{:S(2)}) %collective-permute-start) | collective-permute-done | bytes 262176 | tf_op jit(solution)/shard_map/ppermute | solution.py:16
  23.9 4.3 collective-permute-done.1
  28.2 1.7 pad_maximum_fusion
  29.9 1.9 pad
  31.8 6.8 copy.179
  38.6 1.5 slice.27
  40.2 11.3 %fusion.16 = (f32[2,64,8,9,64]{4,2,3,1,0:T(8,128)S(1)}, f32[2,64,8,9,64]{4,2,3,1,0:T(8,128)}) fusion(f32[64]{0:T(128)S(1)} %copy-done.8, pred[8,9]{0,1:T(8,128)(4,1)S(1)} %copy-done.11, bf16[3,3,3,32,64]{4,3,2,1,0:T(8,128)(2,1)S(1)} %copy-done.6, bf16[4,64,1,7,2,32]{5,3,4,1,0,2:T(8,128)(2,1)S(1)} %slice.27, bf16[4,64,1,8,9,32]{5,3,4,1,0,2:T(8,128)(2,1)} %copy.179), kind=kOutput, calls=%fused_computation.18 | convolution fusion | flops 1018822656 | bytes 6238536 | tf_op jit(solution)/shard_map/conv_general_dilated | solution.py:26
  51.5 0.9 copy.180
  52.4 2.0 slice_reduce_fusion
  54.4 3.3 reduce_sum.36
  57.9 0.3 convert_element_type.57
  58.1 4.5 collective-permute-start.2
  62.8 1.8 collective-permute-start.3
  64.5 5.4 copy.198
  69.9 13.0 %copy.205 = bf16[1,4,64,64,32]{4,0,3,2,1:T(2,128)(2,1)} copy(bf16[1,4,64,64,32]{2,4,3,1,0:T(8,128)(2,1)S(1)} %bitcast.106) | data formatting | bytes 2097152 | tf_op jit(solution)/shard_map/reshape | solution.py:74
  82.9 1.2 concatenate.41
  84.2 0.5 constant_dynamic-update-slice_fusion.1
  84.7 0.6 copy_dynamic-update-slice_fusion
  85.3 1.2 concatenate.42
  86.6 0.6 constant_dynamic-update-slice_fusion
  87.2 0.9 copy.236
  88.3 0.4 copy.188
  88.8 1.5 add_multiply_fusion.1
  90.5 0.3 convert_reduce_fusion.1
  90.9 5.0 collective-permute-start.4
  96.0 1.5 collective-permute-start.5
  97.5 8.1 fusion.56
  105.5 79.7 %psum.47 = f32[128]{0:T(128)} all-reduce(f32[128]{0:T(128)S(1)} %get-tuple-element.35), channel_id=1, replica_groups=mesh['dp'=16,'space'=16] {'dp','space'}, use_global_device_ids=true, to_apply=%region_9.10 | all-reduce | flops 128 | bytes 1024 | tf_op jit(solution)/shard_map/psum | solution.py:90
  185.4 0.3 copy.212
  185.8 0.4 copy.196
  186.3 2.5 fusion.47
  189.0 1.0 broadcast_in_dim.4
  190.1 0.8 fusion.17
  190.9 1.4 copy-done.2
  192.2 1.4 copy.238
  193.6 83.7 %fusion.18 = f32[3,3,3,32,64]{4,3,2,1,0:T(8,128)} fusion(bf16[1,4,64,64,32]{4,0,3,2,1:T(2,128)(2,1)S(1)} %bitcast.116, bf16[1,2,64,64,64]{4,3,2,1,0:T(8,128)(2,1)S(1)} %bitcast.108), kind=kOutput, calls=%fused_computation.25 | convolution fusion | flops 887193600 | bytes 2318336 | tf_op jit(solution)/shard_map/conv_general_dilated | solution.py:37
  277.4 0.5 broadcast_multiply_fusion.2
  278.2 2.5 reshape.107
  280.7 2.3 fusion.71
  282.9 4.8 collective-permute-start.6
  287.7 1.3 collective-permute-start.7
  288.9 2.8 convert_reduce_fusion
  291.8 32.6 %psum.44 = f32[64]{0:T(128)S(1)} all-reduce(f32[64]{0:T(128)S(1)} %convert_reduce_fusion), channel_id=1, replica_groups=mesh['dp'=16,'space'=16] {'dp'}, use_global_device_ids=true, to_apply=%region_5.0 | all-reduce | flops 64 | bytes 512 | tf_op jit(solution)/shard_map/psum | solution.py:106
  324.3 36.3 %psum.45 = f32[64]{0:T(128)S(1)} all-reduce(f32[64]{0:T(128)S(1)} %psum.44), channel_id=1, replica_groups=mesh['dp'=16,'space'=16] {'space'}, use_global_device_ids=true, to_apply=%region_6.0 | all-reduce | flops 64 | bytes 512 | tf_op jit(solution)/shard_map/psum | solution.py:106
  360.7 0.5 broadcast_multiply_fusion.3
  361.2 57.0 %all-reduce.4.cloned.1.call-done = f32[3,3,3,32,64]{4,3,2,1,0:T(8,128)} async-done(((f32[3,3,3,32,64]{4,3,2,1,0:T(8,128)}), f32[3,3,3,32,64]{4,3,2,1,0:T(8,128)}) %all-reduce.4.cloned.1.call-update) | async-done | bytes 221200 | tf_op jit(solution)/shard_map/psum | solution.py:106
  418.3 267.2 %all-reduce.8.cloned.1.call-done = f32[3,3,3,64,128]{4,3,2,1,0:T(8,128)} async-done(((f32[3,3,3,64,128]{4,3,2,1,0:T(8,128)}), f32[3,3,3,64,128]{4,3,2,1,0:T(8,128)}) %all-reduce.8.cloned.1.call-update) | async-done | bytes 884752 | tf_op jit(solution)/shard_map/psum | solution.py:90
  685.4 2.2 broadcast_multiply_fusion
  687.6 133.6 %all-reduce.6.cloned.1.call-done = f32[3,3,3,32,64]{4,3,2,1,0:T(8,128)} async-done(((f32[3,3,3,32,64]{4,3,2,1,0:T(8,128)}), f32[3,3,3,32,64]{4,3,2,1,0:T(8,128)}) %all-reduce.6.cloned.1.call-update) | async-done | bytes 221200 | tf_op jit(solution)/shard_map/psum | solution.py:106
  821.2 1.8 broadcast_multiply_fusion.1
  823.0 2.8 concatenate.34
  825.8 2.1 concatenate.35
  827.9 2.2 maximum_bitcast_fusion
  830.1 2.7 copy.213
  832.9 1.3 pad.6.clone
  834.1 3.0 copy.203
  837.2 0.3 slice.36
  837.5 18.0 %fusion.4 = bf16[2,64,8,9,32]{4,2,3,1,0:T(8,128)(2,1)} fusion(bf16[3,3,3,32,64]{4,3,2,1,0:T(8,128)(2,1)S(1)} %copy-done.7, bf16[4,64,1,7,2,64]{5,3,4,1,0,2:T(8,128)(2,1)S(1)} %slice.36, bf16[4,64,1,8,9,64]{5,3,4,1,0,2:T(8,128)(2,1)S(1)} %copy.203), kind=kOutput, calls=%fused_computation.6 | convolution fusion | flops 1017249792 | bytes 3518464 | tf_op jit(solution)/shard_map/conv_general_dilated | solution.py:48
  855.6 3.2 copy.204
  858.7 0.3 select_convert_fusion
  859.1 1.1 copy.208
  (65 shorter events, 1.9 us)
Async XLA Ops:
  7.2 81.6 %copy-start = (bf16[3,3,3,64,128]{4,3,2,1,0:T(8,128)(2,1)S(1)}, bf16[3,3,3,64,128]{4,3,2,1,0:T(8,128)(2,1)}, u32[]{:S(2)}) copy-start(bf16[3,3,3,64,128]{4,3,2,1,0:T(8,128)(2,1)} %param.9) | copy-start | bytes 1327108
  7.2 411.1 %all-reduce.4.cloned.1.call-start = ((), (), s32[]{:S(2)}) async-start(), calls=%async_computation | async-start | bytes 884736 | tf_op jit(solution)/shard_map/psum | solution.py:106
  8.8 15.1 %copy-start.3 = (bf16[1,2,64,2048]{2,3,1,0:T(8,128)(2,1)}, bf16[1,2,64,2048]{2,3,1,0:T(8,128)(2,1)S(1)}, u32[]{:S(2)}) copy-start(bf16[1,2,64,2048]{2,3,1,0:T(8,128)(2,1)S(1)} %copy.175) | copy-start | bytes 1572868
  8.9 15.0 %collective-permute-start = (bf16[1,1,64,2048]{2,3,1,0:T(8,128)(2,1)S(1)}, bf16[1,1,64,2048]{2,3,1,0:T(8,128)(2,1)S(1)}, u32[]{:S(2)}, u32[]{:S(2)}) collective-permute-start(bf16[1,1,64,2048]{2,3,1,0:T(8,128)(2,1)S(1)} %get-tuple-element.43), channel_id=1, source_target_pairs={{0,1},{1,2},{2,3},{3,4},{4,5},{5,6},{6,7},{7,8},{8,9},{9,10},{10,1... | collective-permute-start | bytes 786440 | tf_op jit(solution)/shard_map/ppermute | solution.py:16
  12.7 15.4 %collective-permute-start.1 = (bf16[1,1,64,2048]{2,3,1,0:T(8,128)(2,1)S(1)}, bf16[1,1,64,2048]{2,3,1,0:T(8,128)(2,1)S(1)}, u32[]{:S(2)}, u32[]{:S(2)}) collective-permute-start(bf16[1,1,64,2048]{2,3,1,0:T(8,128)(2,1)S(1)} %get-tuple-element.44), channel_id=1, source_target_pairs={{1,0},{2,1},{3,2},{4,3},{5,4},{6,5},{7,6},{8,7},{9,8},{10,9},{11,1... | collective-permute-start | bytes 786440 | tf_op jit(solution)/shard_map/ppermute | solution.py:18
  31.8 8.3 copy-start.6
  31.8 8.3 copy-start.8
  31.8 8.3 copy-start.11
  52.4 10.3 %copy-start.4 = (bf16[1,1,32,4096]{3,2,1,0:T(8,128)(2,1)S(1)}, bf16[1,1,32,4096]{3,2,1,0:T(8,128)(2,1)}, u32[]{:S(2)}) copy-start(bf16[1,1,32,4096]{3,2,1,0:T(8,128)(2,1)} %param.11) | copy-start | bytes 786436
  58.1 24.8 %collective-permute-start.2 = (bf16[1,1,32,2048]{3,2,1,0:T(8,128)(2,1)S(1)}, bf16[1,1,32,2048]{3,2,1,0:T(8,128)(2,1)}, u32[]{:S(2)}, u32[]{:S(2)}) collective-permute-start(bf16[1,1,32,2048]{3,2,1,0:T(8,128)(2,1)S(1)} %convert_element_type.57), channel_id=1, source_target_pairs={{0,1},{1,2},{2,3},{3,4},{4,5},{5,6},{6,7},{7,8},{8,9},{9,10},{10,1... | collective-permute-start | bytes 393224 | tf_op jit(solution)/shard_map/ppermute | solution.py:16
  62.8 22.6 %collective-permute-start.3 = (bf16[1,1,32,2048]{3,2,1,0:T(8,128)(2,1)S(1)}, bf16[1,1,32,2048]{3,2,1,0:T(8,128)(2,1)}, u32[]{:S(2)}, u32[]{:S(2)}) collective-permute-start(bf16[1,1,32,2048]{3,2,1,0:T(8,128)(2,1)S(1)} %convert_element_type.57), channel_id=1, source_target_pairs={{1,0},{2,1},{3,2},{4,3},{5,4},{6,5},{7,6},{8,7},{9,8},{10,9},{11,1... | collective-permute-start | bytes 393224 | tf_op jit(solution)/shard_map/ppermute | solution.py:18
  85.3 3.5 copy-start.9
  85.3 3.5 copy-start.12
  90.9 94.3 %collective-permute-start.4 = (bf16[1,1,32,4096]{3,2,1,0:T(8,128)(2,1)S(1)}, bf16[1,1,32,4096]{3,2,1,0:T(8,128)(2,1)S(1)}, u32[]{:S(2)}, u32[]{:S(2)}) collective-permute-start(bf16[1,1,32,4096]{3,2,1,0:T(8,128)(2,1)S(1)} %reshape.106), channel_id=1, source_target_pairs={{0,1},{1,2},{2,3},{3,4},{4,5},{5,6},{6,7},{7,8},{8,9},{9,10},{10,1... | collective-permute-start | bytes 786440 | tf_op jit(solution)/shard_map/ppermute | solution.py:16
  96.0 89.3 %collective-permute-start.5 = (bf16[1,1,32,4096]{3,2,1,0:T(8,128)(2,1)S(1)}, bf16[1,1,32,4096]{3,2,1,0:T(8,128)(2,1)S(1)}, u32[]{:S(2)}, u32[]{:S(2)}) collective-permute-start(bf16[1,1,32,4096]{3,2,1,0:T(8,128)(2,1)S(1)} %reshape.106), channel_id=1, source_target_pairs={{1,0},{2,1},{3,2},{4,3},{5,4},{6,5},{7,6},{8,7},{9,8},{10,9},{11,1... | collective-permute-start | bytes 786440 | tf_op jit(solution)/shard_map/ppermute | solution.py:18
  186.2 3.8 slice-start
  186.3 3.7 slice-start.1
  188.8 4.8 slice-start.2
  190.1 3.6 slice-start.3
  190.9 1.4 copy-start.2
  193.6 83.8 %copy-start.10 = (f32[128]{0:T(128)S(1)}, f32[128]{0:T(128)}, u32[]{:S(2)}) copy-start(f32[128]{0:T(128)} %psum.47) | copy-start | bytes 1540
  277.4 408.0 %all-reduce.8.cloned.1.call-start = ((), (), s32[]{:S(2)}) async-start(), calls=%async_computation.2 | async-start | bytes 1769472 | tf_op jit(solution)/shard_map/psum | solution.py:90
  278.1 543.1 %all-reduce.6.cloned.1.call-start = ((), (), s32[]{:S(2)}) async-start(), calls=%async_computation.1 | async-start | bytes 884736 | tf_op jit(solution)/shard_map/psum | solution.py:106
  282.9 540.1 %collective-permute-start.6 = (bf16[1,1,64,4096]{3,2,1,0:T(8,128)(2,1)}, bf16[1,1,64,4096]{3,2,1,0:T(8,128)(2,1)}, u32[]{:S(2)}, u32[]{:S(2)}) collective-permute-start(bf16[1,1,64,4096]{3,2,1,0:T(8,128)(2,1)} %get-tuple-element.41), channel_id=1, source_target_pairs={{0,1},{1,2},{2,3},{3,4},{4,5},{5,6},{6,7},{7,8},{8,9},{9,10},{10,1... | collective-permute-start | bytes 1572872 | tf_op jit(solution)/shard_map/ppermute | solution.py:16
  287.7 538.2 %collective-permute-start.7 = (bf16[1,1,64,4096]{3,2,1,0:T(8,128)(2,1)}, bf16[1,1,64,4096]{3,2,1,0:T(8,128)(2,1)S(1)}, u32[]{:S(2)}, u32[]{:S(2)}) collective-permute-start(bf16[1,1,64,4096]{3,2,1,0:T(8,128)(2,1)} %get-tuple-element.42), channel_id=1, source_target_pairs={{1,0},{2,1},{3,2},{4,3},{5,4},{6,5},{7,6},{8,7},{9,8},{10,9},{11,1... | collective-permute-start | bytes 1572872 | tf_op jit(solution)/shard_map/ppermute | solution.py:18
  834.1 3.3 copy-start.7
  837.5 21.2 %copy-start.5 = (pred[8,9]{1,0:T(8,128)(4,1)S(1)}, pred[8,9]{1,0:T(8,128)(4,1)}, u32[]{:S(2)}) copy-start(pred[8,9]{1,0:T(8,128)(4,1)} %constant.34) | copy-start | bytes 220
  837.5 22.8 %copy-start.1 = (bf16[3,3,3,64,128]{4,3,2,1,0:T(8,128)(2,1)S(1)}, bf16[3,3,3,64,128]{4,3,2,1,0:T(8,128)(2,1)}, u32[]{:S(2)}) copy-start(bf16[3,3,3,64,128]{4,3,2,1,0:T(8,128)(2,1)} %param.9) | copy-start | bytes 1327108
Sparse Core Ops, SparseCore 0:
  277.5 140.6 all-reduce.3
  424.3 261.0 all-reduce.7
  688.0 133.1 all-reduce.5
